TPU v7x, 512 devices: a whole 4x8x8 slice. The times are simulated.
512 devices in a mesh: dp: 16 (over z_lo, x), tensor: 32 (over z_hi, y, core).
Axes of the slice: x: 4, y: 8, z: 8 (z_hi: 2, z_lo: 4; z = z_hi * 4 + z_lo), core: 2. Of those that a mesh axis runs over, the one named last changes fastest.
Arguments:
- calibration: bfloat16 [4096, 6144], P('dp'), may hold values from -60 to 60
- expert_ids: int32 [4096, 2], P('dp'), may hold values from 0 to 7, all different within a row; in each aligned block of 256 rows (0 to 255, 256 to 511, ...) at most 80 rows name the same one
- chosen_expert: int32 [1], replicated, may hold values from 0 to 7
- ratio_ids: int32 [10], replicated, may hold values from 0 to 19
- gate_weight: bfloat16 [6144, 16384], P('dp', 'tensor'), may hold values from -0.078125 to 0.078125
Outputs:
- col_loss: float32 [10, 16384], P(None, 'tensor')
- losses: float32 [10], replicated
- best_loss: float32 [1], replicated
Inputs may be any that keep to these rules, and one draw needn't show every extreme that they name: `expert_ids`: each row names two different experts; in the rows of one device no expert is named by more than 80 rows, a bound that some block reaches; every expert is named by some row.
All inputs are finite; a program needn't handle non-finite values.
Results may differ from a plain program's by a relative error of at most 0.0044.
Values may be sent and summed in bfloat16 or wider, within the bound.
A program may use at most 128 MiB of HBM per device.

v0:
```python
import math

import jax
import jax.numpy as jnp
from jax import lax
from jax.sharding import PartitionSpec as P

FF = 16384
GRID = 20
GROUP = 128
CAP = 80


LEVELS = 7.0
LOSS_SCALE = 100.0


def copy_for_each(shard, axis):
    copies = jnp.broadcast_to(shard, (lax.axis_size(axis), *shard.shape))
    return lax.all_to_all(copies, axis, split_axis=0, concat_axis=0, tiled=True)


def in_order(tiles, dim):
    tiles = jnp.moveaxis(tiles, 0, dim)
    shape = tiles.shape
    return tiles.reshape(*shape[:dim], shape[dim] * shape[dim + 1], *shape[dim + 2 :])


def collect(shard, axis, dim):
    tiles = copy_for_each(shard, axis)
    return in_order(tiles, dim)


def taken_together(shard, axis):
    everything = copy_for_each(shard, axis)
    return jnp.sum(everything, axis=0)


def pick_rows(expert_rows, block, expert, capacity):
    hit = jnp.any(expert_rows == expert, axis=1)
    position = jnp.cumsum(hit.astype(jnp.int32)) - 1
    slots = jnp.arange(capacity, dtype=jnp.int32)
    selected = hit[None, :] & (position[None, :] == slots[:, None])
    order = jnp.arange(block.shape[0], dtype=jnp.int32)
    row_index = jnp.sum(jnp.where(selected, order[None, :], 0), axis=1)
    occupied = jnp.any(selected, axis=1)
    routed = jnp.where(
        occupied[:, None], jnp.take(block, row_index, axis=0), jnp.zeros((), block.dtype)
    )
    return (routed, occupied)


def error_matrix(weight, channel_sum, ratio):
    exponent = ratio.astype(jnp.float32) / GRID
    scales = jnp.exp(exponent * jnp.log(channel_sum))
    scaled = weight.astype(jnp.float32) * scales[:, None]
    grouped = scaled.reshape(weight.shape[0] // GROUP, GROUP, weight.shape[1])
    step_size = (jnp.max(jnp.abs(grouped), axis=1) + 1e-06) / LEVELS
    phase = grouped / step_size[:, None, :]
    error = -step_size[:, None, :] / (2.0 * math.pi) * jnp.sin(2.0 * math.pi * phase)
    return (error.reshape(weight.shape) / scales[:, None]).astype(jnp.bfloat16)


def body(calibration, expert_ids, chosen_expert, ratio_ids, gate_weight):
    routed, occupied = pick_rows(expert_ids, calibration, chosen_expert[0], CAP)
    gathered, marks = (
        lax.all_gather(routed, "dp", axis=0, tiled=True),
        lax.all_gather(occupied.astype(jnp.bfloat16), "dp", axis=0, tiled=True),
    )
    channel_sum = 0.001 + jnp.sum(jnp.abs(gathered.astype(jnp.float32)), axis=0)
    token_count = jnp.sum(marks.astype(jnp.float32))
    columns = lax.all_to_all(gate_weight, "dp", split_axis=1, concat_axis=0, tiled=True)
    errors = jax.vmap(lambda ratio: error_matrix(columns, channel_sum, ratio))(ratio_ids)
    product = jnp.einsum("td,rdc->rtc", gathered, errors, preferred_element_type=jnp.float32)
    piece = LOSS_SCALE * jnp.sum(product * product, axis=1) / token_count
    col_loss = collect(piece, "dp", 1)
    losses = taken_together(jnp.sum(col_loss, axis=1), "tensor") / FF
    best_loss = jnp.min(losses)[None]
    return (col_loss, losses, best_loss)


def solution(mesh):
    placed = (P("dp", None), P("dp", None), P(), P(), P("dp", "tensor"))
    return jax.shard_map(
        body, mesh=mesh, in_specs=placed, out_specs=(P(None, "tensor"), P(), P()), check_vma=False
    )
```

profile of v0, /device:TPU:1, one launch (start us, length us, event | category | flops | bytes accessed | tf_op | source)
XLA Modules:
  0.0 327.8 jit_solution(977112203842133712)
XLA Ops:
  7.2 0.0 all-gather.2.cloned.1.call-start
  8.0 0.9 compare_reduce_fusion
  9.0 0.3 reduce-window.9
  9.3 0.1 slice.7
  9.4 0.1 slice_reduce_fusion
  9.5 0.1 add_bitcast_fusion
  9.6 0.1 select_reduce_fusion
  9.7 0.1 fusion.12
  9.9 2.1 gather_fusion
  12.0 2.4 select_select_fusion
  14.3 0.0 all-gather.2.cloned.1.call-update
  14.4 0.9 copy.44
  15.3 10.4 %all-to-all-start = ((bf16[384,16,32]{0,2,1:T(8,128)(2,1)}), bf16[384,16,32]{0,2,1:T(8,128)(2,1)S(1)}, u32[]{:S(2)}, u32[]{:S(2)}) async-start(bf16[384,16,32]{0,2,1:T(8,128)(2,1)} %bitcast), calls=%async_computation | async-start | bytes 786432 | tf_op jit(solution)/shard_map/all_to_all | solution.py:72
  25.7 1.3 dynamic-slice
  27.6 0.2 dynamic-update-slice
  27.9 40.5 %all-reduce = bf16[1280]{0:T(1024)(128)(2,1)S(1)} all-reduce(bf16[1280]{0:T(1024)(128)(2,1)S(1)} %dynamic-update-slice), channel_id=1, replica_groups=mesh['dp'=16,'tensor'=32] {'dp'}, use_global_device_ids=true, to_apply=%add | all-reduce | flops 1280 | bytes 5120
  68.3 0.6 convert_reduce_fusion
  69.0 1.1 convert_bitcast_fusion
  70.0 1.4 copy.45
  71.4 2.1 reshape.140
  73.4 2.3 copy.46
  75.7 2.1 copy.52
  77.8 121.8 %all-gather.2.cloned.1.call-done = bf16[1280,6144]{1,0:T(8,128)(2,1)} async-done(((bf16[80,6144]{1,0:T(8,128)(2,1)}), bf16[1280,6144]{1,0:T(8,128)(2,1)}) %all-gather.2.cloned.1.call-update) | async-done | bytes 15728656 | tf_op jit(solution)/shard_map/all_gather | solution.py:67
  199.6 7.0 %abs_reduce_fusion = f32[6144]{0:T(1024)S(1)} fusion(bf16[1280,6144]{1,0:T(8,128)(2,1)} %all-gather.2.cloned.1.call-done), kind=kLoop, calls=%fused_computation.1 | loop fusion | flops 23586816 | bytes 15753216 | tf_op jit(solution)/shard_map/reduce_sum | solution.py:70
  206.6 0.6 add_log_fusion
  207.2 0.1 multiply_exponential_fusion.1
  207.4 2.1 abs_reduce_fusion.1
  209.5 0.1 copy.47
  209.6 0.1 add_multiply_fusion
  209.7 4.9 %div.46 = f32[10,48,128,32]{2,1,3,0:T(8,128)} broadcast(f32[10,48,32]{1,2,0:T(8,128)S(1)} %get-tuple-element.7), dimensions={0,1,3} | broadcast | bytes 7925760 | tf_op jit(solution)/shard_map/vmap()/div | solution.py:59
  214.5 9.0 %div.47 = f32[10,6144,32]{1,2,0:T(8,128)} reshape(f32[10,48,128,32]{2,1,3,0:T(8,128)} %div.46) | data formatting | bytes 15728640 | tf_op jit(solution)/shard_map/vmap()/div | solution.py:59
  223.5 4.9 %mul.79 = f32[10,48,128,32]{2,1,3,0:T(8,128)} broadcast(f32[10,48,32]{1,2,0:T(8,128)S(1)} %get-tuple-element.8), dimensions={0,1,3} | broadcast | bytes 7925760 | tf_op jit(solution)/shard_map/vmap()/mul | solution.py:60
  228.4 9.0 %mul.80 = f32[10,6144,32]{1,2,0:T(8,128)} reshape(f32[10,48,128,32]{2,1,3,0:T(8,128)} %mul.79) | data formatting | bytes 15728640 | tf_op jit(solution)/shard_map/vmap()/mul | solution.py:60
  237.4 0.1 multiply_exponential_fusion
  237.5 35.6 %fusion.8 = f32[10,32]{1,0:T(8,128)S(1)} fusion(bf16[1280,6144]{1,0:T(8,128)(2,1)} %all-gather.2.cloned.1.call-done, f32[10,6144,32]{1,2,0:T(8,128)} %mul.80, f32[10,6144,32]{1,2,0:T(8,128)} %div.47, f32[10,6144]{1,0:T(8,128)S(1)} %multiply_exponential_fusion, f32[6144,32]{0,1:T(8,128)} %bitcast.39), kind=kOutput, calls=%fused_computation.10 | convolution fusion | flops 5045779968 | bytes 32490752 | tf_op jit(solution)/shard_map/td,rdc->rtc/dot_general | solution.py:74
  273.1 0.7 multiply_divide_fusion
  273.8 0.1 reshape.158
  273.9 16.3 %all_to_all.24 = f32[16,1,320]{2,1,0:T(1,128)S(1)} all-to-all(f32[16,1,320]{2,1,0:T(1,128)S(1)} %reshape.158), channel_id=1, replica_groups=mesh['dp'=16,'tensor'=32] {'dp'}, dimensions={0} | all-to-all | bytes 40960 | tf_op jit(solution)/shard_map/all_to_all | solution.py:20
  290.3 0.5 broadcast.125
  290.8 0.7 reduce.6
  291.5 0.1 reshape.159
  291.6 0.1 reduce_sum.61
  291.7 0.6 broadcast_in_dim.62
  292.3 15.7 %all-to-all-start.2 = ((f32[32,1,10]{2,1,0:T(1,128)}), f32[32,1,10]{2,1,0:T(1,128)S(1)}, u32[]{:S(2)}, u32[]{:S(2)}) async-start(f32[32,1,10]{2,1,0:T(1,128)} %broadcast_in_dim.62), calls=%async_computation.2 | async-start | bytes 32768 | tf_op jit(solution)/shard_map/all_to_all | solution.py:20
  308.0 0.7 reshape.139
  308.7 11.0 %all-to-all-done.2 = f32[32,1,10]{2,1,0:T(1,128)S(1)} async-done(((f32[32,1,10]{2,1,0:T(1,128)}), f32[32,1,10]{2,1,0:T(1,128)S(1)}, u32[]{:S(2)}, u32[]{:S(2)}) %all-to-all-start.2) | async-done | bytes 1312 | tf_op jit(solution)/shard_map/all_to_all | solution.py:20
  319.8 0.1 reduce_sum.62
  319.8 1.1 fusion.16
  (25 shorter events, 0.2 us)
Async XLA Ops:
  7.2 2.7 copy-start
  7.2 7.2 %copy-start.2 = (bf16[384,512]{1,0:T(8,128)(2,1)S(1)}, bf16[384,512]{1,0:T(8,128)(2,1)}, u32[]{:S(2)}) copy-start(bf16[384,512]{1,0:T(8,128)(2,1)} %param.9) | copy-start | bytes 1179652
  7.2 192.4 %all-gather.2.cloned.1.call-start = ((), (), s32[]{:S(2)}) async-start(), calls=%async_computation.3 | async-start | bytes 16711680 | tf_op jit(solution)/shard_map/all_gather | solution.py:67
  9.5 59.4 %copy-start.6 = (s32[10]{0:T(128)S(1)}, s32[10]{0:T(128)}, u32[]{:S(2)}) copy-start(s32[10]{0:T(128)} %param.8) | copy-start | bytes 124
  15.3 53.7 %all-to-all-start = ((bf16[384,16,32]{0,2,1:T(8,128)(2,1)}), bf16[384,16,32]{0,2,1:T(8,128)(2,1)S(1)}, u32[]{:S(2)}, u32[]{:S(2)}) async-start(bf16[384,16,32]{0,2,1:T(8,128)(2,1)} %bitcast), calls=%async_computation | async-start | bytes 786432 | tf_op jit(solution)/shard_map/all_to_all | solution.py:72
  69.0 138.3 %copy-start.4 = (f32[10]{0:T(128)}, f32[10]{0:T(128)S(1)}, u32[]{:S(2)}) copy-start(f32[10]{0:T(128)S(1)} %convert_multiply_fusion) | copy-start | bytes 124
  199.6 7.7 %copy-start.1 = (f32[48,128,32]{1,2,0:T(8,128)S(1)}, f32[48,128,32]{1,2,0:T(8,128)}, u32[]{:S(2)}) copy-start(f32[48,128,32]{1,2,0:T(8,128)} %copy.46) | copy-start | bytes 2359300
  228.4 9.0 %copy-start.3 = (f32[6144]{0:T(1024)S(1)}, f32[6144]{0:T(1024)}, u32[]{:S(2)}) copy-start(f32[6144]{0:T(1024)} %get-tuple-element.9) | copy-start | bytes 73732
  228.4 9.0 %copy-start.5 = (f32[10]{0:T(128)S(1)}, f32[10]{0:T(128)}, u32[]{:S(2)}) copy-start(f32[10]{0:T(128)} %copy-done.4) | copy-start | bytes 124
  292.3 27.5 %all-to-all-start.2 = ((f32[32,1,10]{2,1,0:T(1,128)}), f32[32,1,10]{2,1,0:T(1,128)S(1)}, u32[]{:S(2)}, u32[]{:S(2)}) async-start(f32[32,1,10]{2,1,0:T(1,128)} %broadcast_in_dim.62), calls=%async_computation.2 | async-start | bytes 32768 | tf_op jit(solution)/shard_map/all_to_all | solution.py:20
Sparse Core Ops, SparseCore 0:
  14.5 185.0 all-gather.1
where the time goes:
time: 329 us; the launch traced here: 328 us
  waiting for transfers between devices  133 us (40%)
  blocking collectives  56.8 us (17%)
  local copies, waits for them, and re-layouts  42.4 us (13%)
  matrix products  35.6 us (11%)
  starting transfers between devices  26.1 us (8%)
  other arithmetic  18.3 us (6%)
  between operations  15.7 us (5%)
    all_gather x1, waiting for transfers between devices, body(): lax.all_gather(routed, 'dp', axis=0, tiled=True)  122 us
    unnamed x1, blocking collectives  40.5 us
    dot_general x1, matrix products, body(): jnp.einsum('td,rdc->rtc', gathered, errors, preferred_element_type=jnp.fl...  35.6 us
    all_to_all x1, blocking collectives, copy_for_each(): return lax.all_to_all(copies, axis, split_axis=0, concat_axis=0, tiled=True)  16.3 us
    all_to_all x1, starting transfers between devices, copy_for_each(): return lax.all_to_all(copies, axis, split_axis=0, concat_axis=0, tiled=True)  15.7 us
    div x2, local copies, waits for them, and re-layouts, error_matrix(): phase = grouped / step_size[:, None, :]  13.9 us
    mul x2, local copies, waits for them, and re-layouts, error_matrix(): -step_size[:, None, :] / (2.0 * math.pi) * jnp.sin(2.0 * math.pi * phase)  13.9 us
    all_to_all x1, waiting for transfers between devices, copy_for_each(): return lax.all_to_all(copies, axis, split_axis=0, concat_axis=0, tiled=True)  11 us
  transfers between devices with their start and end apart: 3, of which 2 were waited for; matrix products, arithmetic and copies ran while one was open for 4% of the time, Pallas kernels for 0%

commit v1 on v0

v1 whole, which is shorter than its diff:
```python
import functools
import math

import jax
import jax.numpy as jnp
from jax import lax
from jax.experimental import pallas as pl
from jax.experimental.pallas import tpu as pltpu
from jax.sharding import PartitionSpec as P

FF = 16384
GRID = 20
GROUP = 128
CAP = 80
RATIOS = 10
LOSS_SCALE = 100.0
MESH = pl.DeviceIdType.MESH
VMEM = pl.BlockSpec(memory_space=pltpu.VMEM)
SMEM = pl.BlockSpec(memory_space=pltpu.SMEM)
DMA = pltpu.SemaphoreType.DMA

SINE = (
    6.283182818554192,
    -41.34142139892848,
    81.59618387812884,
    -76.58010057012196,
    41.20539503311958,
    -12.271262584796501,
)
SCALED = tuple(-c / (14.0 * math.pi) for c in SINE)


def params(**more):
    return pltpu.CompilerParams(vmem_limit_bytes=62 * 1024 * 1024, **more)


def place():
    dp, tensor = lax.axis_index("dp"), lax.axis_index("tensor")
    zl, x = dp // 4, dp % 4
    zh, y, c = tensor // 16, (tensor // 2) % 8, tensor % 2
    return dp, tensor, zl, x, zh, y, c


def beside(dz):
    dp, tensor, zl, x, zh, y, c = place()
    z = (zh * 4 + zl + dz) % 8
    return {"dp": (z % 4) * 4 + x, "tensor": ((z // 4) * 8 + y) * 2 + c}


def dp_peers():
    return [(dz, dx) for dz in range(4) for dx in range(4) if (dz, dx) != (0, 0)]


def tensor_peers():
    return [(a, b, c) for a in range(2) for b in range(8) for c in range(2) if (a, b, c) != (0, 0, 0)]


def dp_peer(dz, dx):
    dp, tensor, zl, x, zh, y, c = place()
    return {"dp": ((zl + dz) % 4) * 4 + (x + dx) % 4, "tensor": tensor}


def tensor_peer(dh, dy, dc):
    dp, tensor, zl, x, zh, y, c = place()
    return {"dp": dp, "tensor": (((zh + dh) % 2) * 8 + (y + dy) % 8) * 2 + (c + dc) % 2}


def meet(peers):
    barrier = pltpu.get_barrier_semaphore()
    for peer in peers:
        pl.semaphore_signal(barrier, inc=1, device_id=peer, device_id_type=MESH)
    pl.semaphore_wait(barrier, len(peers))


def remote(src, dst, send, recv, peer):
    return pltpu.make_async_remote_copy(
        src_ref=src, dst_ref=dst, send_sem=send, recv_sem=recv, device_id=peer, device_id_type=MESH
    )


def pick_kernel(expert_ref, ids_ref, block_ref, routed_ref, sums_ref):
    tokens, width = block_ref.shape
    hit = jnp.any(ids_ref[...] == expert_ref[0], axis=0, keepdims=True)
    hit = jnp.broadcast_to(jnp.where(hit, 1.0, 0.0), (8, tokens)).astype(jnp.bfloat16)
    up_to = lax.broadcasted_iota(jnp.int32, (tokens, tokens), 0) <= lax.broadcasted_iota(
        jnp.int32, (tokens, tokens), 1
    )
    place_of = jnp.dot(hit, jnp.where(up_to, 1.0, 0.0).astype(jnp.bfloat16), preferred_element_type=jnp.float32)
    slots = lax.broadcasted_iota(jnp.int32, (CAP, tokens), 0).astype(jnp.float32) + 1.0
    wanted = jnp.where(place_of[:1] == slots, hit[:1].astype(jnp.float32), 0.0)
    one_hot = wanted.astype(jnp.bfloat16)
    part = 512

    def pick(k, _):
        at = pl.ds(pl.multiple_of(k * part, part), part)
        rows = jnp.dot(one_hot, block_ref[:, at], preferred_element_type=jnp.float32)
        routed_ref[:, at] = rows.astype(jnp.bfloat16)
        sums_ref[:, at] = jnp.sum(jnp.abs(rows), axis=0, keepdims=True)
        return 0

    lax.fori_loop(0, width // part, pick, 0)
    sums_ref[:, width:] = jnp.broadcast_to(jnp.sum(wanted), (1, 128))


def exchange_kernel(
    routed_ref, sums_ref, w_ref, gath_ref, total_ref, wg_ref, zsum, xsum,
    zs_send, zs_recv, xs_send, xs_recv, w_send, w_recv, g_send, g_recv, d_send, d_recv,
):
    dp, tensor, zl, x, zh, y, c = place()
    width = routed_ref.shape[1]
    half = width // 2
    sibling = tensor_peer(0, 0, 1)
    meet([dp_peer(*o) for o in dp_peers()] + [beside(dz) for dz in (1, 7, 2, 6)] + [sibling])

    sums = [
        remote(sums_ref, zsum.at[zl], zs_send.at[k], zs_recv.at[k], beside(dz))
        for k, dz in enumerate((1, 7, 2))
    ]
    for copy in sums:
        copy.start()
    weights = []
    for k, (dz, dx) in enumerate(dp_peers()):
        columns = pl.ds(pl.multiple_of(((zl + dz) % 4) * GROUP, GROUP), GROUP)
        weights.append(remote(w_ref.at[:, columns], wg_ref.at[dp], w_send.at[k], w_recv.at[k], dp_peer(dz, dx)))
        weights[-1].start()
    rows = []
    low = c * half
    for k, (dz, start, size) in enumerate(((1, 0, half), (7, 0, half), (2, 0, half // 2), (6, half // 2, half // 2))):
        at = pl.ds(pl.multiple_of(low + start, GROUP), size)
        rows.append(remote(routed_ref.at[:, at], gath_ref.at[zl, :, at], g_send.at[k], g_recv.at[k], beside(dz)))
        rows[-1].start()

    zsum[zl] = sums_ref[...]
    for copy in sums:
        copy.wait_recv()
    xsum[x] = ((zsum[0] + zsum[1]) + zsum[2]) + zsum[3]
    across = [
        remote(xsum.at[x], xsum.at[x], xs_send.at[k], xs_recv.at[k], dp_peer(0, dx))
        for k, dx in enumerate((1, 3, 2))
    ]
    for copy in across:
        copy.start()
    gath_ref[zl] = routed_ref[...]
    wg_ref[dp] = w_ref[:, pl.ds(pl.multiple_of(zl * GROUP, GROUP), GROUP)]
    for copy in across:
        copy.wait_recv()
    total_ref[...] = ((xsum[0] + xsum[1]) + xsum[2]) + xsum[3]

    mine = pl.ds(pl.multiple_of(low, GROUP), half)
    passed = []
    for k, (arrived, back) in enumerate((((0,), 3), ((1,), 1), ((2, 3), 2))):
        for one in arrived:
            rows[one].wait_recv()
        held = gath_ref.at[(zl + back) % 4, :, mine]
        passed.append(remote(held, held, d_send.at[k], d_recv.at[k], sibling))
        passed[-1].start()
    for copy in weights:
        copy.wait_recv()
    for copy in passed:
        copy.wait_recv()
    for copy in sums + weights + rows + across + passed:
        copy.wait_send()


def errors_of(w7, aw, s, rs):
    t = jnp.max(aw * s, axis=1, keepdims=True) + 1e-6
    u = (w7 * s) * (1.0 / t)
    x = u - jnp.round(u)
    z = x * x
    p = z * SCALED[5] + SCALED[4]
    for c in SCALED[3::-1]:
        p = p * z + c
    return ((x * t) * rs * p).astype(jnp.bfloat16)


def search_kernel(ratio_ref, g_ref, total_ref, w_ref, out_ref, aw, w7, s_ref, rs_ref, err, acc):
    depth, cols = w_ref.shape
    rows = g_ref.shape[0]
    groups, width = 8, 512

    def turn(k, _):
        at = pl.ds(pl.multiple_of(k * GROUP, GROUP), GROUP)
        tile = w_ref[at, :].astype(jnp.float32).T
        aw[:, at] = jnp.abs(tile)
        w7[:, at] = 7.0 * tile
        return 0

    lax.fori_loop(0, depth // GROUP, turn, 0)
    logs = jnp.log(0.001 + total_ref[:, :depth])
    for r in range(RATIOS):
        s = jnp.exp((ratio_ref[r].astype(jnp.float32) / GRID) * logs)
        s_ref[r] = s
        rs_ref[r] = 1.0 / s

    def fill(i, _):
        r, k = i // (depth // GROUP // groups), i % (depth // GROUP // groups)
        for h in range(groups):
            at = pl.ds(pl.multiple_of((k * groups + h) * GROUP, GROUP), GROUP)
            err[pl.ds(pl.multiple_of(r * cols, cols), cols), at] = errors_of(
                w7[:, at], aw[:, at], s_ref[r, :, at], rs_ref[r, :, at]
            )
        return 0

    lax.fori_loop(0, RATIOS * (depth // GROUP // groups), fill, 0)
    acc[...] = jnp.zeros_like(acc)

    def multiply(k, _):
        at = pl.ds(pl.multiple_of(k * width, GROUP), width)
        acc[...] += lax.dot_general(
            err[:, at], g_ref[:, at], (((1,), (1,)), ((), ())), preferred_element_type=jnp.float32
        )
        return 0

    lax.fori_loop(0, depth // width, multiply, 0)
    factor = LOSS_SCALE / total_ref[:, depth:]
    for r in range(RATIOS):
        a = acc[r * cols : (r + 1) * cols, :]
        a = a * a
        folded = a[:, :128] + a[:, 128:256]
        folded = folded.T
        rest = a[:, 256:rows].T
        out_ref[r : r + 1, :] = factor * (
            jnp.sum(folded, axis=0, keepdims=True) + jnp.sum(rest, axis=0, keepdims=True)
        )
    out_ref[RATIOS:, :] = jnp.zeros((16 - RATIOS, cols), jnp.float32)


def close_kernel(part_ref, col_ref, losses_ref, best_ref, parts, sums, p_send, p_recv, l_send, l_recv):
    dp, tensor, zl, x, zh, y, c = place()
    meet([dp_peer(*o) for o in dp_peers()] + [tensor_peer(*o) for o in tensor_peers()])
    pieces = [
        remote(part_ref, parts.at[dp], p_send.at[k], p_recv.at[k], dp_peer(*o)) for k, o in enumerate(dp_peers())
    ]
    for copy in pieces:
        copy.start()
    parts[dp] = part_ref[...]
    for copy in pieces:
        copy.wait_recv()
    held = jnp.zeros((16, 1), jnp.float32)
    for q in range(4):
        piece = ((parts[4 * q] + parts[4 * q + 1]) + parts[4 * q + 2]) + parts[4 * q + 3]
        col_ref[:, q * 128 : (q + 1) * 128] = piece[:RATIOS]
        held = held + jnp.sum(piece, axis=1, keepdims=True)
    diagonal = lax.broadcasted_iota(jnp.int32, (16, 128), 0) == lax.broadcasted_iota(jnp.int32, (16, 128), 1)
    sums[tensor] = jnp.sum(jnp.where(diagonal, held, 0.0), axis=0, keepdims=True)
    rows = [
        remote(sums.at[tensor], sums.at[tensor], l_send.at[k], l_recv.at[k], tensor_peer(*o))
        for k, o in enumerate(tensor_peers())
    ]
    for copy in rows:
        copy.start()
    for copy in rows:
        copy.wait_recv()
    losses = jnp.sum(sums[...], axis=0) / FF
    losses_ref[...] = losses
    lane = lax.broadcasted_iota(jnp.int32, (1, 128), 1)
    best = jnp.min(jnp.where(lane < RATIOS, losses, jnp.inf), axis=1, keepdims=True)
    best_ref[...] = jnp.broadcast_to(best, (1, 128))
    for copy in pieces + rows:
        copy.wait_send()


def body(calibration, expert_ids, chosen_expert, ratio_ids, gate_weight):
    f32, bf16 = jnp.float32, jnp.bfloat16
    width = calibration.shape[1]
    slab, cols = gate_weight.shape
    long = width + 128
    routed, sums = pl.pallas_call(
        pick_kernel,
        out_shape=[jax.ShapeDtypeStruct((CAP, width), bf16), jax.ShapeDtypeStruct((1, long), f32)],
        in_specs=[SMEM, VMEM, VMEM],
        out_specs=[VMEM, VMEM],
        compiler_params=params(),
        name="pick",
    )(chosen_expert, expert_ids.T, calibration)
    gathered, total, columns = pl.pallas_call(
        exchange_kernel,
        out_shape=[
            jax.ShapeDtypeStruct((4, CAP, width), bf16),
            jax.ShapeDtypeStruct((1, long), f32),
            jax.ShapeDtypeStruct((16, slab, cols // 4), bf16),
        ],
        in_specs=[VMEM] * 3,
        out_specs=[VMEM] * 3,
        scratch_shapes=[
            pltpu.VMEM((4, 1, long), f32), pltpu.VMEM((4, 1, long), f32),
            DMA((3,)), DMA((3,)), DMA((3,)), DMA((3,)), DMA((15,)), DMA((15,)), DMA((4,)), DMA((4,)), DMA((3,)), DMA((3,)),
        ],
        compiler_params=params(collective_id=0, has_side_effects=True),
        name="exchange",
    )(routed, sums, gate_weight)
    part = pl.pallas_call(
        search_kernel,
        out_shape=jax.ShapeDtypeStruct((16, cols // 4), f32),
        in_specs=[SMEM, VMEM, VMEM, VMEM],
        out_specs=VMEM,
        scratch_shapes=[
            pltpu.VMEM((cols // 4, width), f32), pltpu.VMEM((cols // 4, width), f32),
            pltpu.VMEM((RATIOS, 1, width), f32), pltpu.VMEM((RATIOS, 1, width), f32),
            pltpu.VMEM((RATIOS * cols // 4, width), bf16), pltpu.VMEM((RATIOS * cols // 4, 4 * CAP), f32),
        ],
        compiler_params=params(),
        name="search",
    )(ratio_ids, gathered.reshape(4 * CAP, width), total, columns.reshape(16 * slab, cols // 4))
    col_loss, losses, best = pl.pallas_call(
        close_kernel,
        out_shape=[
            jax.ShapeDtypeStruct((RATIOS, cols), f32),
            jax.ShapeDtypeStruct((1, 128), f32),
            jax.ShapeDtypeStruct((1, 128), f32),
        ],
        in_specs=[VMEM],
        out_specs=[VMEM] * 3,
        scratch_shapes=[
            pltpu.VMEM((16, 16, 128), f32), pltpu.VMEM((32, 1, 128), f32),
            DMA((15,)), DMA((15,)), DMA((31,)), DMA((31,)),
        ],
        compiler_params=params(collective_id=1, has_side_effects=True),
        name="close",
    )(part)
    return col_loss, losses[0, :RATIOS], best[0, :1]


def solution(mesh):
    placed = (P("dp", None), P("dp", None), P(), P(), P("dp", "tensor"))
    return jax.shard_map(
        body, mesh=mesh, in_specs=placed, out_specs=(P(None, "tensor"), P(), P()), check_vma=False
    )
```

time: 329 us -> 157 us (0.48)
  Pallas kernels: 0 us -> 152 us
  waiting for transfers between devices: 133 us -> 0 us
  blocking collectives: 56.8 us -> 0 us
  local copies, waits for them, and re-layouts: 42.4 us -> 2.49 us
  matrix products: 35.6 us -> 0 us
  starting transfers between devices: 26.1 us -> 0 us
  other arithmetic: 18.3 us -> 0 us
  between operations: 15.7 us -> 2.98 us
    pallas_call x0 -> x4, Pallas kernels: none -> 152 us  [the longest x1 73.1 us: body(): pl.pallas_call(exchange_kernel, out_shape=[jax.ShapeDtypeStruct((4, CAP,...]
    all_gather x1 -> x0, waiting for transfers between devices: 122 us -> none  [body(): lax.all_gather(routed, 'dp', axis=0, tiled=True)]
    unnamed x1 -> x0, blocking collectives: 40.5 us -> none
    dot_general x1 -> x0, matrix products: 35.6 us -> none  [body(): jnp.einsum('td,rdc->rtc', gathered, errors, preferred_element_type=jnp.fl...]
    all_to_all x2 -> x0, starting transfers between devices: 26 us -> none  [the longest x1 15.7 us: copy_for_each(): return lax.all_to_all(copies, axis, split_axis=0, concat_axis=0, tiled=True)]
    all_to_all x1 -> x0, blocking collectives: 16.3 us -> none  [copy_for_each(): return lax.all_to_all(copies, axis, split_axis=0, concat_axis=0, tiled=True)]
    div x2 -> x0, local copies, waits for them, and re-layouts: 13.9 us -> none  [error_matrix(): phase = grouped / step_size[:, None, :]]
    mul x2 -> x0, local copies, waits for them, and re-layouts: 13.9 us -> none  [error_matrix(): -step_size[:, None, :] / (2.0 * math.pi) * jnp.sin(2.0 * math.pi * phase)]
  transfers between devices with their start and end apart: 3 -> 0, of which waited for: 2 -> 0; matrix products, arithmetic and copies ran while one was open for 4% -> 0% of each run, Pallas kernels for 0% -> 0%
where the time goes in v1:
time: 157 us
  Pallas kernels  152 us (97%)
  between operations  2.98 us (2%)
  local copies, waits for them, and re-layouts  2.49 us (2%)
    pallas_call x1, Pallas kernels, body(): pl.pallas_call(exchange_kernel, out_shape=[jax.ShapeDtypeStruct((4, CAP,...  73.1 us
    pallas_call x1, Pallas kernels, body(): pl.pallas_call(search_kernel, out_shape=jax.ShapeDtypeStruct((16, cols //...  48.2 us
    pallas_call x1, Pallas kernels, body(): pl.pallas_call(close_kernel, out_shape=[jax.ShapeDtypeStruct((RATIOS, col...  25 us
    pallas_call x1, Pallas kernels, body(): pl.pallas_call(pick_kernel, out_shape=[jax.ShapeDtypeStruct((CAP, width),...  5.37 us

profile of v1, /device:TPU:1, one launch (start us, length us, event | category | flops | bytes accessed | tf_op | source)
XLA Modules:
  0.0 157.2 jit_solution(15033957941701689000)
XLA Ops:
  1.3 5.4 %pick.1 = (bf16[80,6144]{1,0:T(8,128)(2,1)}, f32[1,6272]{1,0:T(1,128)}) custom-call(s32[1]{0:T(128)S(6)} %copy.10.expert_ref, s32[2,256]{1,0:T(2,128)} %bitcast.9, bf16[256,6144]{1,0:T(8,128)(2,1)} %block_ref.1), custom_call_target="tpu_custom_call" | custom-call | tf_op jit(solution)/shard_map/pick/pallas_call | solution.py:268
  6.6 73.1 %exchange.1 = (bf16[4,80,6144]{2,1,0:T(8,128)(2,1)}, f32[1,6272]{1,0:T(1,128)}, bf16[16,384,128]{2,1,0:T(8,128)(2,1)}) custom-call(bf16[80,6144]{1,0:T(8,128)(2,1)} %get-tuple-element.11.routed_ref, f32[1,6272]{1,0:T(1,128)} %get-tuple-element.12.sums_ref, bf16[384,512]{1,0:T(8,128)(2,1)} %w_ref.1), custom_call_target="tpu_custom_call" | custom-call | tf_op jit(solution)/shard_map/exchange/pallas_call | solution.py:276
  79.7 48.2 %search.1.part_ref = f32[16,128]{1,0:T(8,128)} custom-call(s32[10]{0:T(128)} %ratio_ref.1, bf16[320,6144]{1,0:T(8,128)(2,1)} %bitcast.7, f32[1,6272]{1,0:T(1,128)} %get-tuple-element.14.total_ref, bf16[6144,128]{1,0:T(8,128)(2,1)} %bitcast.8), custom_call_target="tpu_custom_call" | custom-call | tf_op jit(solution)/shard_map/search/pallas_call | solution.py:292
  128.0 25.0 %close.1 = (f32[10,512]{1,0:T(8,128)}, f32[1,128]{1,0:T(1,128)}, f32[1,128]{1,0:T(1,128)}) custom-call(f32[16,128]{1,0:T(8,128)} %search.1.part_ref), custom_call_target="tpu_custom_call" | custom-call | tf_op jit(solution)/shard_map/close/pallas_call | solution.py:305
  153.0 1.1 slice_bitcast_fusion
  154.1 1.4 copy.11

commit v2 on v0

v2 whole, which is shorter than its diff:
```python
import functools
import math

import jax
import jax.numpy as jnp
from jax import lax
from jax.experimental import pallas as pl
from jax.experimental.pallas import tpu as pltpu
from jax.sharding import PartitionSpec as P

FF = 16384
GRID = 20
GROUP = 128
CAP = 80
RATIOS = 10
LOSS_SCALE = 100.0
MESH = pl.DeviceIdType.MESH
VMEM = pl.BlockSpec(memory_space=pltpu.VMEM)
SMEM = pl.BlockSpec(memory_space=pltpu.SMEM)
DMA = pltpu.SemaphoreType.DMA

SINE = (
    6.283182818554192,
    -41.34142139892848,
    81.59618387812884,
    -76.58010057012196,
    41.20539503311958,
    -12.271262584796501,
)
SCALED = tuple(-c / (14.0 * math.pi) for c in SINE)


def params(**more):
    return pltpu.CompilerParams(vmem_limit_bytes=62 * 1024 * 1024, **more)


def place():
    dp, tensor = lax.axis_index("dp"), lax.axis_index("tensor")
    zl, x = dp // 4, dp % 4
    zh, y, c = tensor // 16, (tensor // 2) % 8, tensor % 2
    return dp, tensor, zl, x, zh, y, c


def beside(dz):
    dp, tensor, zl, x, zh, y, c = place()
    z = (zh * 4 + zl + dz) % 8
    return {"dp": (z % 4) * 4 + x, "tensor": ((z // 4) * 8 + y) * 2 + c}


def dp_peers():
    return [(dz, dx) for dz in range(4) for dx in range(4) if (dz, dx) != (0, 0)]


def tensor_peers():
    return [(a, b, c) for a in range(2) for b in range(8) for c in range(2) if (a, b, c) != (0, 0, 0)]


def dp_peer(dz, dx):
    dp, tensor, zl, x, zh, y, c = place()
    return {"dp": ((zl + dz) % 4) * 4 + (x + dx) % 4, "tensor": tensor}


def tensor_peer(dh, dy, dc):
    dp, tensor, zl, x, zh, y, c = place()
    return {"dp": dp, "tensor": (((zh + dh) % 2) * 8 + (y + dy) % 8) * 2 + (c + dc) % 2}


def remote(src, dst, send, recv, peer):
    return pltpu.make_async_remote_copy(
        src_ref=src, dst_ref=dst, send_sem=send, recv_sem=recv, device_id=peer, device_id_type=MESH
    )


def pick(expert_ref, ids_ref, block_ref, routed_ref, sums_ref):
    tokens, width = block_ref.shape
    hit = jnp.any(ids_ref[...] == expert_ref[0], axis=0, keepdims=True)
    hit = jnp.broadcast_to(jnp.where(hit, 1.0, 0.0), (8, tokens)).astype(jnp.bfloat16)
    up_to = lax.broadcasted_iota(jnp.int32, (tokens, tokens), 0) <= lax.broadcasted_iota(
        jnp.int32, (tokens, tokens), 1
    )
    place_of = jnp.dot(hit, jnp.where(up_to, 1.0, 0.0).astype(jnp.bfloat16), preferred_element_type=jnp.float32)
    slots = lax.broadcasted_iota(jnp.int32, (CAP, tokens), 0).astype(jnp.float32) + 1.0
    wanted = jnp.where(place_of[:1] == slots, hit[:1].astype(jnp.float32), 0.0)
    one_hot = wanted.astype(jnp.bfloat16)
    part = 1536

    def step(k, _):
        at = pl.ds(pl.multiple_of(k * part, part), part)
        rows = jnp.dot(one_hot, block_ref[:, at], preferred_element_type=jnp.float32)
        routed_ref[:, at] = rows.astype(jnp.bfloat16)
        sums_ref[:, at] = jnp.sum(jnp.abs(rows), axis=0, keepdims=True)
        return 0

    lax.fori_loop(0, width // part, step, 0)
    sums_ref[:, width:] = jnp.broadcast_to(jnp.sum(wanted), (1, 128))


def errors_of(w7, aw, s, rs):
    t = jnp.max(aw * s, axis=1, keepdims=True) + 1e-6
    u = (w7 * s) * (1.0 / t)
    x = u - jnp.round(u)
    z = x * x
    p = z * SCALED[5] + SCALED[4]
    for c in SCALED[3::-1]:
        p = p * z + c
    return ((x * t) * rs * p).astype(jnp.bfloat16)


def kernel(
    expert_ref, ratio_ref, ids_ref, block_ref, w_ref, col_ref, losses_ref, best_ref,
    gath, wg, zsum, xsum, aw, w7, s_ref, rs_ref, err, acc, parts, lsum,
    zs_send, zs_recv, xs_send, xs_recv, a_send, a_recv, b_send, b_recv, f_send, f_recv,
    g_send, g_recv, d_send, d_recv, p_send, p_recv, l_send, l_recv,
):
    dp, tensor, zl, x, zh, y, c = place()
    depth = block_ref.shape[1]
    slab, cols = w_ref.shape[0], w_ref.shape[1] // 4
    half = depth // 2
    sibling = tensor_peer(0, 0, 1)
    peers = [dp_peer(*o) for o in dp_peers()] + [beside(dz) for dz in (1, 7, 2, 6)]
    peers += [tensor_peer(*o) for o in tensor_peers()]
    barrier = pltpu.get_barrier_semaphore()
    for peer in peers:
        pl.semaphore_signal(barrier, inc=1, device_id=peer, device_id_type=MESH)

    def rows_of(block):
        return pl.ds(pl.multiple_of(block * CAP, 16), CAP)

    pick(expert_ref, ids_ref, block_ref, gath.at[rows_of(zl)], zsum.at[zl])
    wg[x, zl] = w_ref[:, pl.ds(pl.multiple_of(zl * cols, cols), cols)]
    pl.semaphore_wait(barrier, len(peers))

    sums = [remote(zsum.at[zl], zsum.at[zl], zs_send.at[k], zs_recv.at[k], beside(dz)) for k, dz in enumerate((1, 7, 2))]
    for copy in sums:
        copy.start()
    along = []
    for k, dz in enumerate((1, 3, 2)):
        columns = pl.ds(pl.multiple_of(((zl + dz) % 4) * cols, cols), cols)
        along.append(remote(w_ref.at[:, columns], wg.at[x, zl], a_send.at[k], a_recv.at[k], dp_peer(dz, 0)))
        along[-1].start()
    beyond = {}

    def across(j):
        held = wg.at[x, (zl + j) % 4]
        for k, dx in enumerate((1, 3)):
            beyond[j, dx] = remote(held, held, b_send.at[2 * j + k], b_recv.at[2 * j + k], dp_peer(0, dx))
            beyond[j, dx].start()

    across(0)
    rows = []
    low = c * half
    for k, (dz, start, size) in enumerate(((1, 0, half), (7, 0, half), (2, 0, half // 2), (6, half // 2, half // 2))):
        at = pl.ds(pl.multiple_of(low + start, GROUP), size)
        held = gath.at[rows_of(zl), at]
        rows.append(remote(held, held, g_send.at[k], g_recv.at[k], beside(dz)))
        rows[-1].start()

    for copy in sums:
        copy.wait_recv()
    xsum[x] = ((zsum[0] + zsum[1]) + zsum[2]) + zsum[3]
    over = [remote(xsum.at[x], xsum.at[x], xs_send.at[k], xs_recv.at[k], dp_peer(0, dx)) for k, dx in enumerate((1, 3, 2))]
    for copy in over:
        copy.start()
    for k, dz in ((0, 1), (1, 3), (2, 2)):
        along[k].wait_recv()
        across((4 - dz) % 4)

    def turn(column):
        def step(i, _):
            for h in range(slab // GROUP):
                tile = wg[column, i, h * GROUP : (h + 1) * GROUP, :].astype(jnp.float32).T
                at = pl.ds(pl.multiple_of((i * 4 + column) * slab + h * GROUP, GROUP), GROUP)
                aw[:, at] = jnp.abs(tile)
                w7[:, at] = 7.0 * tile
            return 0

        lax.fori_loop(0, 4, step, 0)

    def fill(column, first, last):
        def step(r, _):
            for i in range(4):
                for h in range(slab // GROUP):
                    at = pl.ds(pl.multiple_of((i * 4 + column) * slab + h * GROUP, GROUP), GROUP)
                    err[pl.ds(pl.multiple_of(r * cols, cols), cols), at] = errors_of(
                        w7[:, at], aw[:, at], s_ref[r, :, at], rs_ref[r, :, at]
                    )
            return 0

        lax.fori_loop(first, last, step, 0)

    turn(x)
    for copy in over:
        copy.wait_recv()
    total = ((xsum[0] + xsum[1]) + xsum[2]) + xsum[3]
    logs = jnp.log(0.001 + total[:, :depth])
    count = total[:, depth:]
    for r in range(RATIOS):
        s = jnp.exp((ratio_ref[r].astype(jnp.float32) / GRID) * logs)
        s_ref[r] = s
        rs_ref[r] = 1.0 / s

    fill(x, 0, 7)
    onward = []
    behind, ahead = (x + 3) % 4, (x + 1) % 4
    for k, (j, dx, column) in enumerate(((0, 1, behind), (1, 1, behind), (2, 3, ahead), (3, 3, ahead))):
        beyond[j, dx].wait_recv()
        held = wg.at[column, (zl + j) % 4]
        onward.append(remote(held, held, f_send.at[k], f_recv.at[k], dp_peer(0, dx)))
        onward[-1].start()
    fill(x, 7, RATIOS)
    for j in (2, 3):
        beyond[j, 1].wait_recv()
    turn(behind)
    fill(behind, 0, RATIOS)
    for j in (0, 1):
        beyond[j, 3].wait_recv()
    turn(ahead)
    fill(ahead, 0, RATIOS)
    mine = pl.ds(pl.multiple_of(low, GROUP), half)
    passed = []

    def pass_on(k, arrived, back):
        for one in arrived:
            rows[one].wait_recv()
        held = gath.at[rows_of((zl + back) % 4), mine]
        passed.append(remote(held, held, d_send.at[k], d_recv.at[k], sibling))
        passed[-1].start()

    pass_on(0, (0,), 3)
    pass_on(1, (1,), 1)
    for copy in onward:
        copy.wait_recv()
    far = (x + 2) % 4
    turn(far)
    fill(far, 0, 7)
    pass_on(2, (2, 3), 2)
    fill(far, 7, RATIOS)
    for copy in passed:
        copy.wait_recv()

    acc[...] = jnp.zeros_like(acc)
    part = depth // 4

    def multiply(k, _):
        at = pl.ds(pl.multiple_of(k * part, part), part)
        acc[...] += lax.dot_general(
            gath[:, at], err[:, at], (((1,), (1,)), ((), ())), preferred_element_type=jnp.float32
        )
        return 0

    lax.fori_loop(0, 4, multiply, 0)
    factor = LOSS_SCALE / count
    own = parts.at[dp]
    for r in range(RATIOS):
        a = acc[:, r * cols : (r + 1) * cols]
        own[r : r + 1, :] = factor * jnp.sum(a * a, axis=0, keepdims=True)
    own[RATIOS:, :] = jnp.zeros((16 - RATIOS, cols), jnp.float32)

    pieces = [remote(own, own, p_send.at[k], p_recv.at[k], dp_peer(*o)) for k, o in enumerate(dp_peers())]
    for copy in pieces:
        copy.start()
    for copy in pieces:
        copy.wait_recv()
    held = jnp.zeros((16, 1), jnp.float32)
    for q in range(4):
        piece = ((parts[4 * q] + parts[4 * q + 1]) + parts[4 * q + 2]) + parts[4 * q + 3]
        col_ref[:, q * cols : (q + 1) * cols] = piece[:RATIOS]
        held = held + jnp.sum(piece, axis=1, keepdims=True)
    diagonal = lax.broadcasted_iota(jnp.int32, (16, 128), 0) == lax.broadcasted_iota(jnp.int32, (16, 128), 1)
    lsum[tensor] = jnp.sum(jnp.where(diagonal, held, 0.0), axis=0, keepdims=True)
    shares = [
        remote(lsum.at[tensor], lsum.at[tensor], l_send.at[k], l_recv.at[k], tensor_peer(*o))
        for k, o in enumerate(tensor_peers())
    ]
    for copy in shares:
        copy.start()
    for copy in shares:
        copy.wait_recv()
    losses = jnp.sum(lsum[...], axis=0) / FF
    losses_ref[...] = losses
    lane = lax.broadcasted_iota(jnp.int32, (1, 128), 1)
    best = jnp.min(jnp.where(lane < RATIOS, losses, jnp.inf), axis=1, keepdims=True)
    best_ref[...] = jnp.broadcast_to(best, (1, 128))
    for copy in sums + along + list(beyond.values()) + rows + over + onward + passed + pieces + shares:
        copy.wait_send()


def body(calibration, expert_ids, chosen_expert, ratio_ids, gate_weight):
    f32, bf16 = jnp.float32, jnp.bfloat16
    width = calibration.shape[1]
    slab, cols = gate_weight.shape
    long, cols = width + 128, cols // 4
    col_loss, losses, best = pl.pallas_call(
        kernel,
        out_shape=[
            jax.ShapeDtypeStruct((RATIOS, 4 * cols), f32),
            jax.ShapeDtypeStruct((1, 128), f32),
            jax.ShapeDtypeStruct((1, 128), f32),
        ],
        in_specs=[SMEM, SMEM, VMEM, VMEM, VMEM],
        out_specs=[VMEM] * 3,
        scratch_shapes=[
            pltpu.VMEM((4 * CAP, width), bf16),
            pltpu.VMEM((4, 4, slab, cols), bf16),
            pltpu.VMEM((4, 1, long), f32),
            pltpu.VMEM((4, 1, long), f32),
            pltpu.VMEM((cols, width), f32),
            pltpu.VMEM((cols, width), f32),
            pltpu.VMEM((RATIOS, 1, width), f32),
            pltpu.VMEM((RATIOS, 1, width), f32),
            pltpu.VMEM((RATIOS * cols, width), bf16),
            pltpu.VMEM((4 * CAP, RATIOS * cols), f32),
            pltpu.VMEM((16, 16, cols), f32),
            pltpu.VMEM((32, 1, 128), f32),
        ]
        + [DMA((n,)) for n in (3, 3, 3, 3, 3, 3, 8, 8, 4, 4, 4, 4, 3, 3, 15, 15, 31, 31)],
        compiler_params=params(collective_id=0, has_side_effects=True),
        name="search",
    )(chosen_expert, ratio_ids, expert_ids.T, calibration, gate_weight)
    return col_loss, losses[0, :RATIOS], best[0, :1]


def solution(mesh):
    placed = (P("dp", None), P("dp", None), P(), P(), P("dp", "tensor"))
    return jax.shard_map(
        body, mesh=mesh, in_specs=placed, out_specs=(P(None, "tensor"), P(), P()), check_vma=False
    )
```

time: 329 us -> 84.7 us (0.26)
  waiting for transfers between devices: 133 us -> 0 us
  Pallas kernels: 0 us -> 78.9 us
  blocking collectives: 56.8 us -> 0 us
  local copies, waits for them, and re-layouts: 42.4 us -> 2.55 us
  matrix products: 35.6 us -> 0 us
  starting transfers between devices: 26.1 us -> 0 us
  other arithmetic: 18.3 us -> 0 us
  between operations: 15.7 us -> 3.02 us
    all_gather x1 -> x0, waiting for transfers between devices: 122 us -> none  [body(): lax.all_gather(routed, 'dp', axis=0, tiled=True)]
    pallas_call x0 -> x1, Pallas kernels: none -> 78.9 us  [body(): pl.pallas_call(kernel, out_shape=[jax.ShapeDtypeStruct((RATIOS, 4 * cols)...]
    unnamed x1 -> x0, blocking collectives: 40.5 us -> none
    dot_general x1 -> x0, matrix products: 35.6 us -> none  [body(): jnp.einsum('td,rdc->rtc', gathered, errors, preferred_element_type=jnp.fl...]
    all_to_all x2 -> x0, starting transfers between devices: 26 us -> none  [the longest x1 15.7 us: copy_for_each(): return lax.all_to_all(copies, axis, split_axis=0, concat_axis=0, tiled=True)]
    all_to_all x1 -> x0, blocking collectives: 16.3 us -> none  [copy_for_each(): return lax.all_to_all(copies, axis, split_axis=0, concat_axis=0, tiled=True)]
    div x2 -> x0, local copies, waits for them, and re-layouts: 13.9 us -> none  [error_matrix(): phase = grouped / step_size[:, None, :]]
    mul x2 -> x0, local copies, waits for them, and re-layouts: 13.9 us -> none  [error_matrix(): -step_size[:, None, :] / (2.0 * math.pi) * jnp.sin(2.0 * math.pi * phase)]
  transfers between devices with their start and end apart: 3 -> 0, of which waited for: 2 -> 0; matrix products, arithmetic and copies ran while one was open for 4% -> 0% of each run, Pallas kernels for 0% -> 0%
where the time goes in v2:
time: 84.7 us; the launch traced here: 84.5 us
  Pallas kernels  78.9 us (93%)
  between operations  3.02 us (4%)
  local copies, waits for them, and re-layouts  2.55 us (3%)
    pallas_call x1, Pallas kernels, body(): pl.pallas_call(kernel, out_shape=[jax.ShapeDtypeStruct((RATIOS, 4 * cols)...  78.9 us

profile of v2, /device:TPU:1, one launch (start us, length us, event | category | flops | bytes accessed | tf_op | source)
XLA Modules:
  0.0 84.5 jit_solution(1518708863180834354)
XLA Ops:
  1.3 78.9 %search.1 = (f32[10,512]{1,0:T(8,128)}, f32[1,128]{1,0:T(1,128)}, f32[1,128]{1,0:T(1,128)}) custom-call(s32[1]{0:T(128)S(6)} %copy.10.expert_ref, s32[10]{0:T(128)} %ratio_ref.1, s32[2,256]{1,0:T(2,128)} %bitcast.5, bf16[256,6144]{1,0:T(8,128)(2,1)} %block_ref.1, bf16[384,512]{1,0:T(8,128)(2,1)} %w_ref.1), custom_call_target="tpu_custom_call" | custom-call | tf_op jit(solution)/shard_map/search/pallas_call | solution.py:293
  80.2 1.2 %slice_bitcast_fusion = f32[10]{0:T(128)} fusion(f32[1,128]{1,0:T(1,128)} %get-tuple-element.7), kind=kLoop, calls=%fused_computation | loop fusion | bytes 80 | tf_op jit(solution)/shard_map/squeeze | solution.py:320
  81.4 1.4 %copy.11 = f32[10,512]{1,0:T(8,128)} copy(f32[10,512]{1,0:T(8,128)} %get-tuple-element.12) | data formatting | bytes 40960

commit v3 on v2

--- a/solution.py
+++ b/solution.py
@@ -1,4 +1,4 @@
-import functools
+import itertools
 import math
 
 import jax
@@ -17,6 +17,7 @@
 MESH = pl.DeviceIdType.MESH
 VMEM = pl.BlockSpec(memory_space=pltpu.VMEM)
 SMEM = pl.BlockSpec(memory_space=pltpu.SMEM)
+ANY = pl.BlockSpec(memory_space=pl.ANY)
 DMA = pltpu.SemaphoreType.DMA
 
 SINE = (
@@ -41,18 +42,14 @@
     return dp, tensor, zl, x, zh, y, c
 
 
-def beside(dz):
+def others(*sizes):
+    return [o for o in itertools.product(*(range(n) for n in sizes)) if any(o)]
+
+
+def plane_peer(dz, dx):
     dp, tensor, zl, x, zh, y, c = place()
     z = (zh * 4 + zl + dz) % 8
-    return {"dp": (z % 4) * 4 + x, "tensor": ((z // 4) * 8 + y) * 2 + c}
-
-
-def dp_peers():
-    return [(dz, dx) for dz in range(4) for dx in range(4) if (dz, dx) != (0, 0)]
-
-
-def tensor_peers():
-    return [(a, b, c) for a in range(2) for b in range(8) for c in range(2) if (a, b, c) != (0, 0, 0)]
+    return {"dp": (z % 4) * 4 + (x + dx) % 4, "tensor": ((z // 4) * 8 + y) * 2 + c}
 
 
 def dp_peer(dz, dx):
@@ -60,9 +57,9 @@
     return {"dp": ((zl + dz) % 4) * 4 + (x + dx) % 4, "tensor": tensor}
 
 
-def tensor_peer(dh, dy, dc):
+def line_peer(dy, dc):
     dp, tensor, zl, x, zh, y, c = place()
-    return {"dp": dp, "tensor": (((zh + dh) % 2) * 8 + (y + dy) % 8) * 2 + (c + dc) % 2}
+    return {"dp": dp, "tensor": (zh * 8 + (y + dy) % 8) * 2 + (c + dc) % 2}
 
 
 def remote(src, dst, send, recv, peer):
@@ -71,7 +68,7 @@
     )
 
 
-def pick(expert_ref, ids_ref, block_ref, routed_ref, sums_ref):
+def pick(expert_ref, ids_ref, block_ref, loads, routed_ref, sums_ref):
     tokens, width = block_ref.shape
     hit = jnp.any(ids_ref[...] == expert_ref[0], axis=0, keepdims=True)
     hit = jnp.broadcast_to(jnp.where(hit, 1.0, 0.0), (8, tokens)).astype(jnp.bfloat16)
@@ -82,16 +79,13 @@
     slots = lax.broadcasted_iota(jnp.int32, (CAP, tokens), 0).astype(jnp.float32) + 1.0
     wanted = jnp.where(place_of[:1] == slots, hit[:1].astype(jnp.float32), 0.0)
     one_hot = wanted.astype(jnp.bfloat16)
-    part = 1536
-
-    def step(k, _):
-        at = pl.ds(pl.multiple_of(k * part, part), part)
+    part = width // len(loads)
+    for k, load in enumerate(loads):
+        load.wait()
+        at = pl.ds(k * part, part)
         rows = jnp.dot(one_hot, block_ref[:, at], preferred_element_type=jnp.float32)
         routed_ref[:, at] = rows.astype(jnp.bfloat16)
         sums_ref[:, at] = jnp.sum(jnp.abs(rows), axis=0, keepdims=True)
-        return 0
-
-    lax.fori_loop(0, width // part, step, 0)
     sums_ref[:, width:] = jnp.broadcast_to(jnp.sum(wanted), (1, 128))
 
 
@@ -107,30 +101,39 @@
 
 
 def kernel(
-    expert_ref, ratio_ref, ids_ref, block_ref, w_ref, col_ref, losses_ref, best_ref,
-    gath, wg, zsum, xsum, aw, w7, s_ref, rs_ref, err, acc, parts, lsum,
+    expert_ref, ratio_ref, ids_ref, block_hbm, w_hbm, col_ref, losses_ref, best_ref,
+    block_ref, w_ref, gath, wg, zsum, xsum, aw, w7, s_ref, rs_ref, err, acc, parts, plane, line,
+    load_sem,
     zs_send, zs_recv, xs_send, xs_recv, a_send, a_recv, b_send, b_recv, f_send, f_recv,
-    g_send, g_recv, d_send, d_recv, p_send, p_recv, l_send, l_recv,
+    g_send, g_recv, d_send, d_recv, p_send, p_recv, l_send, l_recv, m_send, m_recv,
 ):
     dp, tensor, zl, x, zh, y, c = place()
     depth = block_ref.shape[1]
     slab, cols = w_ref.shape[0], w_ref.shape[1] // 4
     half = depth // 2
-    sibling = tensor_peer(0, 0, 1)
-    peers = [dp_peer(*o) for o in dp_peers()] + [beside(dz) for dz in (1, 7, 2, 6)]
-    peers += [tensor_peer(*o) for o in tensor_peers()]
+    sibling = line_peer(0, 1)
+    peers = [plane_peer(*o) for o in others(8, 4)] + [line_peer(*o) for o in others(8, 2)]
     barrier = pltpu.get_barrier_semaphore()
     for peer in peers:
         pl.semaphore_signal(barrier, inc=1, device_id=peer, device_id_type=MESH)
+    part = depth // 4
+    loads = [
+        pltpu.make_async_copy(block_hbm.at[:, pl.ds(k * part, part)], block_ref.at[:, pl.ds(k * part, part)], load_sem.at[k])
+        for k in range(4)
+    ]
+    weights = pltpu.make_async_copy(w_hbm, w_ref, load_sem.at[4])
+    for load in loads + [weights]:
+        load.start()
 
     def rows_of(block):
         return pl.ds(pl.multiple_of(block * CAP, 16), CAP)
 
-    pick(expert_ref, ids_ref, block_ref, gath.at[rows_of(zl)], zsum.at[zl])
+    pick(expert_ref, ids_ref, block_ref, loads, gath.at[rows_of(zl)], zsum.at[zl])
+    weights.wait()
     wg[x, zl] = w_ref[:, pl.ds(pl.multiple_of(zl * cols, cols), cols)]
     pl.semaphore_wait(barrier, len(peers))
 
-    sums = [remote(zsum.at[zl], zsum.at[zl], zs_send.at[k], zs_recv.at[k], beside(dz)) for k, dz in enumerate((1, 7, 2))]
+    sums = [remote(zsum.at[zl], zsum.at[zl], zs_send.at[k], zs_recv.at[k], plane_peer(dz, 0)) for k, dz in enumerate((1, 7, 2))]
     for copy in sums:
         copy.start()
     along = []
@@ -146,24 +149,24 @@
             beyond[j, dx] = remote(held, held, b_send.at[2 * j + k], b_recv.at[2 * j + k], dp_peer(0, dx))
             beyond[j, dx].start()
 
+    for copy in sums:
+        copy.wait_recv()
+    xsum[x] = ((zsum[0] + zsum[1]) + zsum[2]) + zsum[3]
+    over = [remote(xsum.at[x], xsum.at[x], xs_send.at[k], xs_recv.at[k], dp_peer(0, dx)) for k, dx in enumerate((1, 3, 2))]
+    for copy in over:
+        copy.start()
     across(0)
+    for k, dz in ((0, 1), (1, 3), (2, 2)):
+        along[k].wait_recv()
+        across((4 - dz) % 4)
+
     rows = []
     low = c * half
     for k, (dz, start, size) in enumerate(((1, 0, half), (7, 0, half), (2, 0, half // 2), (6, half // 2, half // 2))):
         at = pl.ds(pl.multiple_of(low + start, GROUP), size)
         held = gath.at[rows_of(zl), at]
-        rows.append(remote(held, held, g_send.at[k], g_recv.at[k], beside(dz)))
+        rows.append(remote(held, held, g_send.at[k], g_recv.at[k], plane_peer(dz, 0)))
         rows[-1].start()
-
-    for copy in sums:
-        copy.wait_recv()
-    xsum[x] = ((zsum[0] + zsum[1]) + zsum[2]) + zsum[3]
-    over = [remote(xsum.at[x], xsum.at[x], xs_send.at[k], xs_recv.at[k], dp_peer(0, dx)) for k, dx in enumerate((1, 3, 2))]
-    for copy in over:
-        copy.start()
-    for k, dz in ((0, 1), (1, 3), (2, 2)):
-        along[k].wait_recv()
-        across((4 - dz) % 4)
 
     def turn(column):
         def step(i, _):
@@ -256,32 +259,35 @@
         own[r : r + 1, :] = factor * jnp.sum(a * a, axis=0, keepdims=True)
     own[RATIOS:, :] = jnp.zeros((16 - RATIOS, cols), jnp.float32)
 
-    pieces = [remote(own, own, p_send.at[k], p_recv.at[k], dp_peer(*o)) for k, o in enumerate(dp_peers())]
+    pieces = [remote(own, own, p_send.at[k], p_recv.at[k], dp_peer(*o)) for k, o in enumerate(others(4, 4))]
     for copy in pieces:
         copy.start()
+    diagonal = lax.broadcasted_iota(jnp.int32, (16, 128), 0) == lax.broadcasted_iota(jnp.int32, (16, 128), 1)
+    row = plane.at[(zh * 4 + zl) * 4 + x]
+    row[...] = jnp.sum(jnp.where(diagonal, jnp.sum(own[...], axis=1, keepdims=True), 0.0), axis=0, keepdims=True)
+    shares = [remote(row, row, l_send.at[k], l_recv.at[k], plane_peer(*o)) for k, o in enumerate(others(8, 4))]
+    for copy in shares:
+        copy.start()
+    for copy in shares:
+        copy.wait_recv()
+    row = line.at[y * 2 + c]
+    row[...] = jnp.sum(plane[...], axis=0)
+    ends = [remote(row, row, m_send.at[k], m_recv.at[k], line_peer(*o)) for k, o in enumerate(others(8, 2))]
+    for copy in ends:
+        copy.start()
     for copy in pieces:
         copy.wait_recv()
-    held = jnp.zeros((16, 1), jnp.float32)
     for q in range(4):
         piece = ((parts[4 * q] + parts[4 * q + 1]) + parts[4 * q + 2]) + parts[4 * q + 3]
         col_ref[:, q * cols : (q + 1) * cols] = piece[:RATIOS]
-        held = held + jnp.sum(piece, axis=1, keepdims=True)
-    diagonal = lax.broadcasted_iota(jnp.int32, (16, 128), 0) == lax.broadcasted_iota(jnp.int32, (16, 128), 1)
-    lsum[tensor] = jnp.sum(jnp.where(diagonal, held, 0.0), axis=0, keepdims=True)
-    shares = [
-        remote(lsum.at[tensor], lsum.at[tensor], l_send.at[k], l_recv.at[k], tensor_peer(*o))
-        for k, o in enumerate(tensor_peers())
-    ]
-    for copy in shares:
-        copy.start()
-    for copy in shares:
-        copy.wait_recv()
-    losses = jnp.sum(lsum[...], axis=0) / FF
+    for copy in ends:
+        copy.wait_recv()
+    losses = jnp.sum(line[...], axis=0) / FF
     losses_ref[...] = losses
     lane = lax.broadcasted_iota(jnp.int32, (1, 128), 1)
     best = jnp.min(jnp.where(lane < RATIOS, losses, jnp.inf), axis=1, keepdims=True)
     best_ref[...] = jnp.broadcast_to(best, (1, 128))
-    for copy in sums + along + list(beyond.values()) + rows + over + onward + passed + pieces + shares:
+    for copy in sums + along + list(beyond.values()) + rows + over + onward + passed + pieces + shares + ends:
         copy.wait_send()
 
 
@@ -297,9 +303,11 @@
             jax.ShapeDtypeStruct((1, 128), f32),
             jax.ShapeDtypeStruct((1, 128), f32),
         ],
-        in_specs=[SMEM, SMEM, VMEM, VMEM, VMEM],
+        in_specs=[SMEM, SMEM, VMEM, ANY, ANY],
         out_specs=[VMEM] * 3,
         scratch_shapes=[
+            pltpu.VMEM(calibration.shape, bf16),
+            pltpu.VMEM((slab, 4 * cols), bf16),
             pltpu.VMEM((4 * CAP, width), bf16),
             pltpu.VMEM((4, 4, slab, cols), bf16),
             pltpu.VMEM((4, 1, long), f32),
@@ -312,8 +320,9 @@
             pltpu.VMEM((4 * CAP, RATIOS * cols), f32),
             pltpu.VMEM((16, 16, cols), f32),
             pltpu.VMEM((32, 1, 128), f32),
+            pltpu.VMEM((16, 1, 128), f32),
         ]
-        + [DMA((n,)) for n in (3, 3, 3, 3, 3, 3, 8, 8, 4, 4, 4, 4, 3, 3, 15, 15, 31, 31)],
+        + [DMA((n,)) for n in (5, 3, 3, 3, 3, 3, 3, 8, 8, 4, 4, 4, 4, 3, 3, 15, 15, 31, 31, 15, 15)],
         compiler_params=params(collective_id=0, has_side_effects=True),
         name="search",
     )(chosen_expert, ratio_ids, expert_ids.T, calibration, gate_weight)

time: 84.7 us -> 82.8 us (0.978)
  Pallas kernels: 78.9 us -> 77 us
    pallas_call x1, Pallas kernels: 78.9 us -> 77 us  [body(): pl.pallas_call(kernel, out_shape=[jax.ShapeDtypeStruct((RATIOS, 4 * cols)...]
where the time goes in v3:
time: 82.8 us; the launch traced here: 82.5 us
  Pallas kernels  77 us (93%)
  between operations  3.02 us (4%)
  local copies, waits for them, and re-layouts  2.55 us (3%)
    pallas_call x1, Pallas kernels, body(): pl.pallas_call(kernel, out_shape=[jax.ShapeDtypeStruct((RATIOS, 4 * cols)...  77 us

profile of v3, /device:TPU:1, one launch (start us, length us, event | category | flops | bytes accessed | tf_op | source)
XLA Modules:
  0.0 82.5 jit_solution(3737914426831083433)
XLA Ops:
  1.3 77.0 %search.1 = (f32[10,512]{1,0:T(8,128)}, f32[1,128]{1,0:T(1,128)}, f32[1,128]{1,0:T(1,128)}) custom-call(s32[1]{0:T(128)S(6)} %copy.10.expert_ref, s32[10]{0:T(128)} %ratio_ref.1, s32[2,256]{1,0:T(2,128)} %bitcast.5, bf16[256,6144]{1,0:T(8,128)(2,1)} %block_hbm.1, bf16[384,512]{1,0:T(8,128)(2,1)} %w_hbm.1), custom_call_target="tpu_custom_call" | custom-call | tf_op jit(solution)/shard_map/search/pallas_call | solution.py:299
  78.2 1.2 %slice_bitcast_fusion = f32[10]{0:T(128)} fusion(f32[1,128]{1,0:T(1,128)} %get-tuple-element.7), kind=kLoop, calls=%fused_computation | loop fusion | bytes 80 | tf_op jit(solution)/shard_map/squeeze | solution.py:329
  79.4 1.4 %copy.11 = f32[10,512]{1,0:T(8,128)} copy(f32[10,512]{1,0:T(8,128)} %get-tuple-element.12) | data formatting | bytes 40960

commit v4 on v3

--- a/solution.py
+++ b/solution.py
@@ -28,7 +28,8 @@
     41.20539503311958,
     -12.271262584796501,
 )
-SCALED = tuple(-c / (14.0 * math.pi) for c in SINE)
+MONIC = tuple(c / SINE[-1] for c in SINE[:-1])
+LEADING = -SINE[-1] / (14.0 * math.pi)
 
 
 def params(**more):
@@ -94,8 +95,8 @@
     u = (w7 * s) * (1.0 / t)
     x = u - jnp.round(u)
     z = x * x
-    p = z * SCALED[5] + SCALED[4]
-    for c in SCALED[3::-1]:
+    p = z + MONIC[-1]
+    for c in MONIC[-2::-1]:
         p = p * z + c
     return ((x * t) * rs * p).astype(jnp.bfloat16)
 
@@ -180,13 +181,16 @@
         lax.fori_loop(0, 4, step, 0)
 
     def fill(column, first, last):
-        def step(r, _):
-            for i in range(4):
-                for h in range(slab // GROUP):
-                    at = pl.ds(pl.multiple_of((i * 4 + column) * slab + h * GROUP, GROUP), GROUP)
-                    err[pl.ds(pl.multiple_of(r * cols, cols), cols), at] = errors_of(
-                        w7[:, at], aw[:, at], s_ref[r, :, at], rs_ref[r, :, at]
-                    )
+        def step(pair, _):
+            for one in range(2):
+                r = pair * 2 + one
+                for i in range(4):
+                    for h in range(slab // GROUP):
+                        group = (i * 4 + column) * (slab // GROUP) + h
+                        at = pl.ds(pl.multiple_of(group * GROUP, GROUP), GROUP)
+                        err[group, pl.ds(pl.multiple_of(r * cols, cols), cols), :] = errors_of(
+                            w7[:, at], aw[:, at], s_ref[r, :, at], rs_ref[r, :, at]
+                        )
             return 0
 
         lax.fori_loop(first, last, step, 0)
@@ -200,9 +204,9 @@
     for r in range(RATIOS):
         s = jnp.exp((ratio_ref[r].astype(jnp.float32) / GRID) * logs)
         s_ref[r] = s
-        rs_ref[r] = 1.0 / s
-
-    fill(x, 0, 7)
+        rs_ref[r] = LEADING / s
+
+    fill(x, 0, 3)
     onward = []
     behind, ahead = (x + 3) % 4, (x + 1) % 4
     for k, (j, dx, column) in enumerate(((0, 1, behind), (1, 1, behind), (2, 3, ahead), (3, 3, ahead))):
@@ -210,15 +214,15 @@
         held = wg.at[column, (zl + j) % 4]
         onward.append(remote(held, held, f_send.at[k], f_recv.at[k], dp_peer(0, dx)))
         onward[-1].start()
-    fill(x, 7, RATIOS)
+    fill(x, 3, RATIOS // 2)
     for j in (2, 3):
         beyond[j, 1].wait_recv()
     turn(behind)
-    fill(behind, 0, RATIOS)
+    fill(behind, 0, RATIOS // 2)
     for j in (0, 1):
         beyond[j, 3].wait_recv()
     turn(ahead)
-    fill(ahead, 0, RATIOS)
+    fill(ahead, 0, RATIOS // 2)
     mine = pl.ds(pl.multiple_of(low, GROUP), half)
     passed = []
 
@@ -235,23 +239,25 @@
         copy.wait_recv()
     far = (x + 2) % 4
     turn(far)
-    fill(far, 0, 7)
+    fill(far, 0, 3)
     pass_on(2, (2, 3), 2)
-    fill(far, 7, RATIOS)
-    for copy in passed:
-        copy.wait_recv()
-
+    fill(far, 3, RATIOS // 2)
     acc[...] = jnp.zeros_like(acc)
-    part = depth // 4
 
     def multiply(k, _):
-        at = pl.ds(pl.multiple_of(k * part, part), part)
+        chunk = (k + 2 * c) % 4
+        at = pl.ds(pl.multiple_of(chunk * part, part), part)
+        groups = part // GROUP
+        errors = jnp.concatenate([err[chunk * groups + j] for j in range(groups)], axis=1)
         acc[...] += lax.dot_general(
-            gath[:, at], err[:, at], (((1,), (1,)), ((), ())), preferred_element_type=jnp.float32
+            gath[:, at], errors, (((1,), (1,)), ((), ())), preferred_element_type=jnp.float32
         )
         return 0
 
-    lax.fori_loop(0, 4, multiply, 0)
+    lax.fori_loop(0, 2, multiply, 0)
+    for copy in passed:
+        copy.wait_recv()
+    lax.fori_loop(2, 4, multiply, 0)
     factor = LOSS_SCALE / count
     own = parts.at[dp]
     for r in range(RATIOS):
@@ -289,6 +295,13 @@
     best_ref[...] = jnp.broadcast_to(best, (1, 128))
     for copy in sums + along + list(beyond.values()) + rows + over + onward + passed + pieces + shares + ends:
         copy.wait_send()
+
+
+def finish_kernel(col_ref, losses_ref, best_ref, col_out, losses_out, best_out):
+    col_out[...] = col_ref[...]
+    for r in range(RATIOS):
+        losses_out[r] = losses_ref[0, r]
+    best_out[0] = best_ref[0, 0]
 
 
 def body(calibration, expert_ids, chosen_expert, ratio_ids, gate_weight):
@@ -316,7 +329,7 @@
             pltpu.VMEM((cols, width), f32),
             pltpu.VMEM((RATIOS, 1, width), f32),
             pltpu.VMEM((RATIOS, 1, width), f32),
-            pltpu.VMEM((RATIOS * cols, width), bf16),
+            pltpu.VMEM((width // GROUP, RATIOS * cols, GROUP), bf16),
             pltpu.VMEM((4 * CAP, RATIOS * cols), f32),
             pltpu.VMEM((16, 16, cols), f32),
             pltpu.VMEM((32, 1, 128), f32),
@@ -326,7 +339,17 @@
         compiler_params=params(collective_id=0, has_side_effects=True),
         name="search",
     )(chosen_expert, ratio_ids, expert_ids.T, calibration, gate_weight)
-    return col_loss, losses[0, :RATIOS], best[0, :1]
+    return pl.pallas_call(
+        finish_kernel,
+        out_shape=[
+            jax.ShapeDtypeStruct((RATIOS, 4 * cols), f32),
+            jax.ShapeDtypeStruct((RATIOS,), f32),
+            jax.ShapeDtypeStruct((1,), f32),
+        ],
+        in_specs=[VMEM, SMEM, SMEM],
+        out_specs=[VMEM, SMEM, SMEM],
+        name="finish",
+    )(col_loss, losses, best)
 
 
 def solution(mesh):

time: 82.8 us -> 77.5 us (0.936)
  local copies, waits for them, and re-layouts: 2.55 us -> 0 us
  between operations: 3.02 us -> 1.29 us
  Pallas kernels: 77 us -> 76 us
    pallas_call x1, Pallas kernels: 77 us -> 74.5 us  [body(): pl.pallas_call(kernel, out_shape=[jax.ShapeDtypeStruct((RATIOS, 4 * cols)...]
    pallas_call x0 -> x1, Pallas kernels: none -> 1.44 us  [body(): pl.pallas_call(finish_kernel, out_shape=[jax.ShapeDtypeStruct((RATIOS, 4...]
    unnamed x1 -> x0, local copies, waits for them, and re-layouts: 1.37 us -> none
    squeeze x1 -> x0, local copies, waits for them, and re-layouts: 1.18 us -> none  [body(): return (col_loss, losses[0, :RATIOS], best[0, :1])]
where the time goes in v4:
time: 77.5 us; the launch traced here: 77.2 us
  Pallas kernels  76 us (98%)
  between operations  1.29 us (2%)
    pallas_call x1, Pallas kernels, body(): pl.pallas_call(kernel, out_shape=[jax.ShapeDtypeStruct((RATIOS, 4 * cols)...  74.5 us

profile of v4, /device:TPU:1, one launch (start us, length us, event | category | flops | bytes accessed | tf_op | source)
XLA Modules:
  0.0 77.2 jit_solution(14587247758269942236)
XLA Ops:
  1.3 74.5 %search.1 = (f32[10,512]{1,0:T(8,128)}, f32[1,128]{1,0:T(1,128)}, f32[1,128]{1,0:T(1,128)}) custom-call(s32[1]{0:T(128)S(6)} %copy.8.expert_ref, s32[10]{0:T(128)} %ratio_ref.1, s32[2,256]{1,0:T(2,128)} %bitcast.1, bf16[256,6144]{1,0:T(8,128)(2,1)} %block_hbm.1, bf16[384,512]{1,0:T(8,128)(2,1)} %w_hbm.1), custom_call_target="tpu_custom_call" | custom-call | tf_op jit(solution)/shard_map/search/pallas_call | solution.py:312
  75.8 1.4 %finish.1 = (f32[10,512]{1,0:T(8,128)}, f32[10]{0:T(128)}, f32[1]{0:T(128)}) custom-call(f32[10,512]{1,0:T(8,128)} %get-tuple-element.6.col_ref, f32[1,128]{1,0:T(1,128)} %get-tuple-element.7.losses_ref, f32[1,128]{1,0:T(1,128)} %get-tuple-element.8.best_ref), custom_call_target="tpu_custom_call" | custom-call | tf_op jit(solution)/shard_map/finish/pallas_call | solution.py:342

commit v5 on v4

--- a/solution.py
+++ b/solution.py
@@ -157,6 +157,7 @@
     for copy in over:
         copy.start()
     across(0)
+    acc[...] = jnp.zeros_like(acc)
     for k, dz in ((0, 1), (1, 3), (2, 2)):
         along[k].wait_recv()
         across((4 - dz) % 4)
@@ -242,8 +243,6 @@
     fill(far, 0, 3)
     pass_on(2, (2, 3), 2)
     fill(far, 3, RATIOS // 2)
-    acc[...] = jnp.zeros_like(acc)
-
     def multiply(k, _):
         chunk = (k + 2 * c) % 4
         at = pl.ds(pl.multiple_of(chunk * part, part), part)
@@ -266,13 +265,11 @@
     own[RATIOS:, :] = jnp.zeros((16 - RATIOS, cols), jnp.float32)
 
     pieces = [remote(own, own, p_send.at[k], p_recv.at[k], dp_peer(*o)) for k, o in enumerate(others(4, 4))]
-    for copy in pieces:
-        copy.start()
     diagonal = lax.broadcasted_iota(jnp.int32, (16, 128), 0) == lax.broadcasted_iota(jnp.int32, (16, 128), 1)
     row = plane.at[(zh * 4 + zl) * 4 + x]
     row[...] = jnp.sum(jnp.where(diagonal, jnp.sum(own[...], axis=1, keepdims=True), 0.0), axis=0, keepdims=True)
     shares = [remote(row, row, l_send.at[k], l_recv.at[k], plane_peer(*o)) for k, o in enumerate(others(8, 4))]
-    for copy in shares:
+    for copy in shares + pieces:
         copy.start()
     for copy in shares:
         copy.wait_recv()

time: 77.5 us -> 76.6 us (0.988)
  Pallas kernels: 76 us -> 75.1 us
    pallas_call x1, Pallas kernels: 74.5 us -> 73.6 us  [body(): pl.pallas_call(kernel, out_shape=[jax.ShapeDtypeStruct((RATIOS, 4 * cols)...]
where the time goes in v5:
time: 76.6 us; the launch traced here: 76.4 us
  Pallas kernels  75.1 us (98%)
  between operations  1.29 us (2%)
    pallas_call x1, Pallas kernels, body(): pl.pallas_call(kernel, out_shape=[jax.ShapeDtypeStruct((RATIOS, 4 * cols)...  73.6 us

profile of v5, /device:TPU:1, one launch (start us, length us, event | category | flops | bytes accessed | tf_op | source)
XLA Modules:
  0.0 76.4 jit_solution(900453353229948466)
XLA Ops:
  1.3 73.6 %search.1 = (f32[10,512]{1,0:T(8,128)}, f32[1,128]{1,0:T(1,128)}, f32[1,128]{1,0:T(1,128)}) custom-call(s32[1]{0:T(128)S(6)} %copy.8.expert_ref, s32[10]{0:T(128)} %ratio_ref.1, s32[2,256]{1,0:T(2,128)} %bitcast.1, bf16[256,6144]{1,0:T(8,128)(2,1)} %block_hbm.1, bf16[384,512]{1,0:T(8,128)(2,1)} %w_hbm.1), custom_call_target="tpu_custom_call" | custom-call | tf_op jit(solution)/shard_map/search/pallas_call | solution.py:309
  74.9 1.4 %finish.1 = (f32[10,512]{1,0:T(8,128)}, f32[10]{0:T(128)}, f32[1]{0:T(128)}) custom-call(f32[10,512]{1,0:T(8,128)} %get-tuple-element.6.col_ref, f32[1,128]{1,0:T(1,128)} %get-tuple-element.7.losses_ref, f32[1,128]{1,0:T(1,128)} %get-tuple-element.8.best_ref), custom_call_target="tpu_custom_call" | custom-call | tf_op jit(solution)/shard_map/finish/pallas_call | solution.py:339

commit v6 on v5

--- a/solution.py
+++ b/solution.py
@@ -44,7 +44,8 @@
 
 
 def others(*sizes):
-    return [o for o in itertools.product(*(range(n) for n in sizes)) if any(o)]
+    offsets = [o for o in itertools.product(*(range(n) for n in sizes)) if any(o)]
+    return sorted(offsets, key=lambda o: -sum(min(i, n - i) for i, n in zip(o, sizes)))
 
 
 def plane_peer(dz, dx):
@@ -113,10 +114,6 @@
     slab, cols = w_ref.shape[0], w_ref.shape[1] // 4
     half = depth // 2
     sibling = line_peer(0, 1)
-    peers = [plane_peer(*o) for o in others(8, 4)] + [line_peer(*o) for o in others(8, 2)]
-    barrier = pltpu.get_barrier_semaphore()
-    for peer in peers:
-        pl.semaphore_signal(barrier, inc=1, device_id=peer, device_id_type=MESH)
     part = depth // 4
     loads = [
         pltpu.make_async_copy(block_hbm.at[:, pl.ds(k * part, part)], block_ref.at[:, pl.ds(k * part, part)], load_sem.at[k])
@@ -125,23 +122,27 @@
     weights = pltpu.make_async_copy(w_hbm, w_ref, load_sem.at[4])
     for load in loads + [weights]:
         load.start()
+    peers = [plane_peer(*o) for o in others(8, 4)] + [line_peer(*o) for o in others(8, 2)]
+    barrier = pltpu.get_barrier_semaphore()
+    for peer in peers:
+        pl.semaphore_signal(barrier, inc=1, device_id=peer, device_id_type=MESH)
 
     def rows_of(block):
         return pl.ds(pl.multiple_of(block * CAP, 16), CAP)
 
     pick(expert_ref, ids_ref, block_ref, loads, gath.at[rows_of(zl)], zsum.at[zl])
-    weights.wait()
-    wg[x, zl] = w_ref[:, pl.ds(pl.multiple_of(zl * cols, cols), cols)]
     pl.semaphore_wait(barrier, len(peers))
 
-    sums = [remote(zsum.at[zl], zsum.at[zl], zs_send.at[k], zs_recv.at[k], plane_peer(dz, 0)) for k, dz in enumerate((1, 7, 2))]
+    sums = [remote(zsum.at[zl], zsum.at[zl], zs_send.at[k], zs_recv.at[k], plane_peer(dz, 0)) for k, dz in enumerate((2, 1, 7))]
     for copy in sums:
         copy.start()
+    weights.wait()
     along = []
     for k, dz in enumerate((1, 3, 2)):
         columns = pl.ds(pl.multiple_of(((zl + dz) % 4) * cols, cols), cols)
         along.append(remote(w_ref.at[:, columns], wg.at[x, zl], a_send.at[k], a_recv.at[k], dp_peer(dz, 0)))
         along[-1].start()
+    wg[x, zl] = w_ref[:, pl.ds(pl.multiple_of(zl * cols, cols), cols)]
     beyond = {}
 
     def across(j):
@@ -153,7 +154,7 @@
     for copy in sums:
         copy.wait_recv()
     xsum[x] = ((zsum[0] + zsum[1]) + zsum[2]) + zsum[3]
-    over = [remote(xsum.at[x], xsum.at[x], xs_send.at[k], xs_recv.at[k], dp_peer(0, dx)) for k, dx in enumerate((1, 3, 2))]
+    over = [remote(xsum.at[x], xsum.at[x], xs_send.at[k], xs_recv.at[k], dp_peer(0, dx)) for k, dx in enumerate((2, 1, 3))]
     for copy in over:
         copy.start()
     across(0)

time: 76.6 us -> 76.5 us (level)
  no operation moved by 1% of the time
where the time goes in v6:
time: 76.5 us; the launch traced here: 76.3 us
  Pallas kernels  75 us (98%)
  between operations  1.29 us (2%)
    pallas_call x1, Pallas kernels, body(): pl.pallas_call(kernel, out_shape=[jax.ShapeDtypeStruct((RATIOS, 4 * cols)...  73.6 us

profile of v6, /device:TPU:1, one launch (start us, length us, event | category | flops | bytes accessed | tf_op | source)
XLA Modules:
  0.0 76.3 jit_solution(17065057607101492645)
XLA Ops:
  1.3 73.6 %search.1 = (f32[10,512]{1,0:T(8,128)}, f32[1,128]{1,0:T(1,128)}, f32[1,128]{1,0:T(1,128)}) custom-call(s32[1]{0:T(128)S(6)} %copy.8.expert_ref, s32[10]{0:T(128)} %ratio_ref.1, s32[2,256]{1,0:T(2,128)} %bitcast.1, bf16[256,6144]{1,0:T(8,128)(2,1)} %block_hbm.1, bf16[384,512]{1,0:T(8,128)(2,1)} %w_hbm.1), custom_call_target="tpu_custom_call" | custom-call | tf_op jit(solution)/shard_map/search/pallas_call | solution.py:310
  74.9 1.4 %finish.1 = (f32[10,512]{1,0:T(8,128)}, f32[10]{0:T(128)}, f32[1]{0:T(128)}) custom-call(f32[10,512]{1,0:T(8,128)} %get-tuple-element.6.col_ref, f32[1,128]{1,0:T(1,128)} %get-tuple-element.7.losses_ref, f32[1,128]{1,0:T(1,128)} %get-tuple-element.8.best_ref), custom_call_target="tpu_custom_call" | custom-call | tf_op jit(solution)/shard_map/finish/pallas_call | solution.py:340

commit v7 on v6

--- a/solution.py
+++ b/solution.py
@@ -172,15 +172,12 @@
         rows[-1].start()
 
     def turn(column):
-        def step(i, _):
+        for i in range(4):
             for h in range(slab // GROUP):
                 tile = wg[column, i, h * GROUP : (h + 1) * GROUP, :].astype(jnp.float32).T
                 at = pl.ds(pl.multiple_of((i * 4 + column) * slab + h * GROUP, GROUP), GROUP)
                 aw[:, at] = jnp.abs(tile)
                 w7[:, at] = 7.0 * tile
-            return 0
-
-        lax.fori_loop(0, 4, step, 0)
 
     def fill(column, first, last):
         def step(pair, _):

time: 76.5 us -> 76.3 us (level)
  no operation moved by 1% of the time
where the time goes in v7:
time: 76.3 us; the launch traced here: 76.1 us
  Pallas kernels  74.8 us (98%)
  between operations  1.29 us (2%)
    pallas_call x1, Pallas kernels, body(): pl.pallas_call(kernel, out_shape=[jax.ShapeDtypeStruct((RATIOS, 4 * cols)...  73.4 us

profile of v7, /device:TPU:1, one launch (start us, length us, event | category | flops | bytes accessed | tf_op | source)
XLA Modules:
  0.0 76.1 jit_solution(1933300914479618237)
XLA Ops:
  1.3 73.4 %search.1 = (f32[10,512]{1,0:T(8,128)}, f32[1,128]{1,0:T(1,128)}, f32[1,128]{1,0:T(1,128)}) custom-call(s32[1]{0:T(128)S(6)} %copy.8.expert_ref, s32[10]{0:T(128)} %ratio_ref.1, s32[2,256]{1,0:T(2,128)} %bitcast.1, bf16[256,6144]{1,0:T(8,128)(2,1)} %block_hbm.1, bf16[384,512]{1,0:T(8,128)(2,1)} %w_hbm.1), custom_call_target="tpu_custom_call" | custom-call | tf_op jit(solution)/shard_map/search/pallas_call | solution.py:307
  74.6 1.4 %finish.1 = (f32[10,512]{1,0:T(8,128)}, f32[10]{0:T(128)}, f32[1]{0:T(128)}) custom-call(f32[10,512]{1,0:T(8,128)} %get-tuple-element.6.col_ref, f32[1,128]{1,0:T(1,128)} %get-tuple-element.7.losses_ref, f32[1,128]{1,0:T(1,128)} %get-tuple-element.8.best_ref), custom_call_target="tpu_custom_call" | custom-call | tf_op jit(solution)/shard_map/finish/pallas_call | solution.py:337
